TPU v7x, 32 devices: a whole 2x2x4 slice. The times are simulated.
32 devices in a mesh: rows: 4 (over y, x), cols: 8 (over z, core).
Axes of the slice: x: 2, y: 2, z: 4, core: 2. Of those that a mesh axis runs over, the one named last changes fastest.
Arguments:
- object_field: float32 [2, 1024, 2048], P(None, 'rows', 'cols'), may hold values from -6 to 6
- probe: float32 [2, 256, 256], replicated, may hold values from -6 to 6
- positions: int32 [4, 8, 6, 2], P('rows', 'cols'), may hold values from 0 to 256
- counts: int32 [4, 8], P('rows', 'cols'), may hold values from 2 to 6
- intensity: int32 [4, 8, 6, 256, 256], P('rows', 'cols'), may hold values from 0 to 4000
Outputs:
- updated_field: float32 [2, 1024, 2048], P(None, 'rows', 'cols')
Inputs may be any that keep to these rules, and one draw needn't show every extreme that they name: Only the first counts[a, b] entries of tile (a, b) in positions and intensity are used.
All inputs are finite; a program needn't handle non-finite values.
Results may differ from a plain program's by a relative error of at most 0.00029.
Values sent between devices are 32-bit elements; how exact they have to be, the bound alone decides.
A program may use at most 64 MiB of HBM per device.

v0:
```python
import functools

import jax
import jax.numpy as jnp
import numpy as np
from jax import lax
from jax.experimental import pallas as pl
from jax.experimental.pallas import tpu as pltpu
from jax.sharding import PartitionSpec as P

MARGIN = 128
ITERS = 2
LANES = 128
ROWS = 8


step_rate = 0.02
photon_unit = 0.001


def extended(block, sides, width):
    for axis, dim in sides:
        count = lax.axis_size(axis)
        forward = [(i, i + 1) for i in range(count - 1)]
        backward = [(target, source) for source, target in forward]
        low = lax.ppermute(
            lax.slice_in_dim(block, block.shape[dim] - width, None, axis=dim), axis, forward
        )
        high = lax.ppermute(lax.slice_in_dim(block, 0, width, axis=dim), axis, backward)
        block = jnp.concatenate([low, block, high], axis=dim)
    return block


def from_behind(block, axis, distance):
    devices = range(lax.axis_size(axis))
    route = [(i - distance, i) for i in devices if i - distance in devices]
    return lax.ppermute(block, axis, route)


def tables(length):
    half = length // 2
    k = np.arange(half)[:, None]
    n = np.arange(half)[None, :]
    found = []
    for odd in (0, 1):
        angle = ((2 * k + odd) * n % length) * (2.0 * np.pi / length)
        c = np.cos(angle) / np.sqrt(length)
        s = np.sin(angle) / np.sqrt(length)
        full = np.block([[c, s], [-s, c]])
        found += [full, full.T]
    full = np.stack(found).astype(np.float32)
    high = full.astype(jnp.bfloat16)
    low = (full - high.astype(np.float32)).astype(jnp.bfloat16)
    return np.stack([high, low])


def ordering(length):
    half = length // 2
    index = np.arange(half)
    table = np.zeros((length, length), np.float32)
    table[2 * index, index] = 1
    table[2 * index + 1, half + index] = 1
    return np.stack([table, table.T]).astype(jnp.bfloat16)


def dot(left, right):
    return lax.dot_general(left, right, (((1,), (0,)), ((), ())), preferred_element_type=jnp.float32)


def parted(value):
    high = value.astype(jnp.bfloat16)
    return high, (value - high.astype(jnp.float32)).astype(jnp.bfloat16)


def from_left(table, which, value):
    high, low = parted(value)
    return dot(table[0, which], high) + dot(table[1, which], high) + dot(table[0, which], low)


def from_right(table, which, value):
    high, low = parted(value)
    return dot(high, table[0, which]) + dot(high, table[1, which]) + dot(low, table[0, which])


def order_kernel(counts_ref, order_ref, intensity_ref, out_ref):
    @pl.loop(0, counts_ref[0, 0])
    def _(slot):
        given = intensity_ref[slot]

        def placed(value):
            value = value.astype(jnp.float32).astype(jnp.bfloat16)
            return dot(dot(order_ref[1], value).astype(jnp.bfloat16), order_ref[0])

        out_ref[slot] = (placed(given >> 4) * 16.0 + placed(given & 15)) * photon_unit


def moved_up(value, shift):
    rows, columns = value.shape
    groups = value.reshape(rows // ROWS, ROWS, columns)
    turned = pltpu.roll(groups, (ROWS - shift) % ROWS, 1)
    within = lax.broadcasted_iota(jnp.int32, (1, ROWS, columns), 1) < ROWS - shift
    return jnp.where(within, turned[:-1], turned[1:]).reshape(rows - ROWS, columns)


def moved_down(value, shift):
    rows, columns = value.shape
    groups = value.reshape(rows // ROWS, ROWS, columns)
    turned = pltpu.roll(groups, shift % ROWS, 1)
    none = jnp.zeros((1, ROWS, columns), value.dtype)
    within = lax.broadcasted_iota(jnp.int32, (1, ROWS, columns), 1) >= shift
    lower = jnp.concatenate([turned, none], axis=0)
    upper = jnp.concatenate([none, turned], axis=0)
    return jnp.where(within, lower, upper).reshape(rows + ROWS, columns)


def moved_left(value, shift):
    rows, columns = value.shape
    parts = [pltpu.roll(value[:, c : c + LANES], (LANES - shift) % LANES, 1) for c in range(0, columns, LANES)]
    within = lax.broadcasted_iota(jnp.int32, (rows, LANES), 1) < LANES - shift
    return jnp.concatenate([jnp.where(within, a, b) for a, b in zip(parts[:-1], parts[1:])], axis=1)


def moved_right(value, shift):
    rows, columns = value.shape
    parts = [pltpu.roll(value[:, c : c + LANES], shift % LANES, 1) for c in range(0, columns, LANES)]
    within = lax.broadcasted_iota(jnp.int32, (rows, LANES), 1) >= shift
    none = jnp.zeros((rows, LANES), value.dtype)
    return jnp.concatenate([jnp.where(within, a, b) for a, b in zip(parts + [none], [none] + parts)], axis=1)


def slots_kernel(positions_ref, counts_ref, padded_ref, probe_ref, measured_ref, table_ref, grad_ref):
    size = probe_ref.shape[1]
    half = size // 2
    wide = size + LANES
    last = padded_ref.shape[1] - size - ROWS
    grad_ref[...] = jnp.zeros_like(grad_ref)

    @pl.loop(0, counts_ref[0, 0])
    def _(slot):
        row = positions_ref[slot, 0]
        column = positions_ref[slot, 1]
        start = pl.multiple_of(jnp.where(column >= LANES, LANES, 0), LANES)
        shift = column - start
        first = pl.multiple_of(jnp.minimum(row // ROWS * ROWS, last), ROWS)
        drop = row - first
        there = (pl.ds(first, size + ROWS), pl.ds(start, wide))
        patch_r = moved_left(moved_up(padded_ref[(0, *there)], drop), shift)
        patch_i = moved_left(moved_up(padded_ref[(1, *there)], drop), shift)
        probe_r = probe_ref[0]
        probe_i = probe_ref[1]
        exit_r = probe_r * patch_r - probe_i * patch_i
        exit_i = probe_r * patch_i + probe_i * patch_r
        upper = jnp.concatenate([exit_r[:half], exit_i[:half]], axis=0)
        lower = jnp.concatenate([exit_r[half:], exit_i[half:]], axis=0)
        even = from_left(table_ref, 0, upper + lower)
        odd = from_left(table_ref, 2, upper - lower)
        half_r = jnp.concatenate([even[:half], odd[:half]], axis=0)
        half_i = jnp.concatenate([even[half:], odd[half:]], axis=0)
        left = jnp.concatenate([half_r[:, :half], half_i[:, :half]], axis=1)
        right = jnp.concatenate([half_r[:, half:], half_i[:, half:]], axis=1)
        backs = []
        for odd, value in ((0, left + right), (1, left - right)):
            spec = from_right(table_ref, 2 * odd + 1, value)
            spec_r, spec_i = spec[:, :half], spec[:, half:]
            misfit = spec_r * spec_r + spec_i * spec_i - measured_ref[slot, :, odd * half : (odd + 1) * half]
            scaled = jnp.concatenate([misfit * spec_r, misfit * spec_i], axis=1)
            backs.append(from_right(table_ref, 2 * odd, scaled))
        left = backs[0] + backs[1]
        right = backs[0] - backs[1]
        half_r = jnp.concatenate([left[:, :half], right[:, :half]], axis=1)
        half_i = jnp.concatenate([left[:, half:], right[:, half:]], axis=1)
        even = from_left(table_ref, 1, jnp.concatenate([half_r[:half], half_i[:half]], axis=0))
        odd = from_left(table_ref, 3, jnp.concatenate([half_r[half:], half_i[half:]], axis=0))
        upper = even + odd
        lower = even - odd
        back_r = jnp.concatenate([upper[:half], lower[:half]], axis=0)
        back_i = jnp.concatenate([upper[half:], lower[half:]], axis=0)
        term_r = probe_r * back_r + probe_i * back_i
        term_i = probe_r * back_i - probe_i * back_r
        for part, term in ((0, term_r), (1, term_i)):
            grad_ref[(part, *there)] += moved_down(moved_right(term, shift), drop)


def in_order(counts, intensity, order):
    slots, size, _ = intensity.shape
    return pl.pallas_call(
        order_kernel,
        out_shape=jax.ShapeDtypeStruct((slots, size, size), jnp.float32),
        in_specs=[pl.BlockSpec(memory_space=pltpu.SMEM)] + [pl.BlockSpec(memory_space=pltpu.VMEM)] * 2,
        out_specs=pl.BlockSpec(memory_space=pltpu.VMEM),
        cost_estimate=pl.CostEstimate(
            flops=slots * 4 * size**3, bytes_accessed=slots * 8 * size**2, transcendentals=0
        ),
        name="order",
    )(counts, order, intensity)


def slot_terms(positions, counts, padded, probe, measured, table):
    slots, size, _ = measured.shape
    return pl.pallas_call(
        slots_kernel,
        out_shape=jax.ShapeDtypeStruct(padded.shape, jnp.float32),
        in_specs=[pl.BlockSpec(memory_space=pltpu.SMEM)] * 2 + [pl.BlockSpec(memory_space=pltpu.VMEM)] * 4,
        out_specs=pl.BlockSpec(memory_space=pltpu.VMEM),
        cost_estimate=pl.CostEstimate(
            flops=slots * 48 * size**3, bytes_accessed=slots * 40 * size**2, transcendentals=0
        ),
        compiler_params=pltpu.CompilerParams(vmem_limit_bytes=48 * 1024 * 1024),
        name="slots",
    )(positions, counts, padded, probe, measured, table)


def on_device(object_field, probe, positions, counts, intensity):
    tile = object_field.shape[1]
    size = probe.shape[1]
    table = jnp.asarray(tables(size))
    order = jnp.asarray(ordering(size))
    positions = positions[0, 0]
    measured = in_order(counts, intensity[0, 0], order)
    field = object_field
    for step in range(ITERS):
        padded = extended(field, (("rows", 1), ("cols", 2)), MARGIN)
        grad = slot_terms(positions, counts, padded, probe, measured, table)
        low = MARGIN
        high = MARGIN + tile
        from_right_side = from_behind(grad[:, :, :low], "cols", -1)
        from_left_side = from_behind(grad[:, :, high:], "cols", 1)
        middle = grad[:, :, low:high]
        middle = middle.at[:, :, tile - low :].add(from_right_side)
        middle = middle.at[:, :, :low].add(from_left_side)
        from_below = from_behind(middle[:, :low, :], "rows", -1)
        from_above = from_behind(middle[:, high:, :], "rows", 1)
        owned = middle[:, low:high, :]
        owned = owned.at[:, tile - low :, :].add(from_below)
        owned = owned.at[:, :low, :].add(from_above)
        field = field - step_rate * owned
    return field


def solution(mesh):
    placed = (
        P(None, "rows", "cols"),
        P(),
        P("rows", "cols", None, None),
        P("rows", "cols"),
        P("rows", "cols", None, None, None),
    )
    return jax.shard_map(
        on_device, mesh=mesh, in_specs=placed, out_specs=P(None, "rows", "cols"), check_vma=False
    )
```

profile of v0, /device:TPU:12, one launch (start us, length us, event | category | flops | bytes accessed | tf_op | source)
XLA Modules:
  0.0 144.4 jit_solution(943122493107614196)
XLA Ops:
  1.1 3.4 %collective-permute-start = (f32[2,128,256]{2,1,0:T(8,128)S(1)}, f32[2,128,256]{2,1,0:T(8,128)S(1)}, u32[]{:S(2)}, u32[]{:S(2)}) collective-permute-start(f32[2,128,256]{2,1,0:T(8,128)S(1)} %get-tuple-element.116), channel_id=1, source_target_pairs={{0,8},{8,16},{16,24},{1,9},{9,17},{17,25},{2,10},{10,18},{18,26},{... | collective-permute-start | bytes 786440 | tf_op jit(solution)/shard_map/ppermute | solution.py:26
  4.5 3.3 %collective-permute-start.1 = (f32[2,128,256]{2,1,0:T(8,128)S(1)}, f32[2,128,256]{2,1,0:T(8,128)S(1)}, u32[]{:S(2)}, u32[]{:S(2)}) collective-permute-start(f32[2,128,256]{2,1,0:T(8,128)S(1)} %get-tuple-element.115), channel_id=1, source_target_pairs={{8,0},{16,8},{24,16},{9,1},{17,9},{25,17},{10,2},{18,10},{26,18},{... | collective-permute-start | bytes 786440 | tf_op jit(solution)/shard_map/ppermute | solution.py:29
  7.8 5.2 %collective-permute-done = f32[2,128,256]{2,1,0:T(8,128)S(1)} collective-permute-done((f32[2,128,256]{2,1,0:T(8,128)S(1)}, f32[2,128,256]{2,1,0:T(8,128)S(1)}, u32[]{:S(2)}, u32[]{:S(2)}) %collective-permute-start) | collective-permute-done | bytes 262176 | tf_op jit(solution)/shard_map/ppermute | solution.py:26
  15.7 1.9 %collective-permute-start.2 = (f32[2,512,128]{2,1,0:T(8,128)S(1)}, f32[2,512,128]{2,1,0:T(8,128)S(1)}, u32[]{:S(2)}, u32[]{:S(2)}) collective-permute-start(f32[2,512,128]{2,1,0:T(8,128)S(1)} %get-tuple-element.111), channel_id=1, source_target_pairs={{0,1},{1,2},{2,3},{3,4},{4,5},{5,6},{6,7},{8,9},{9,10},{10,11},{11... | collective-permute-start | bytes 1572872 | tf_op jit(solution)/shard_map/ppermute | solution.py:26
  17.7 3.6 %collective-permute-start.3 = (f32[2,512,128]{2,1,0:T(8,128)S(1)}, f32[2,512,128]{2,1,0:T(8,128)S(1)}, u32[]{:S(2)}, u32[]{:S(2)}) collective-permute-start(f32[2,512,128]{2,1,0:T(8,128)S(1)} %get-tuple-element.112), channel_id=1, source_target_pairs={{1,0},{2,1},{3,2},{4,3},{5,4},{6,5},{7,6},{9,8},{10,9},{11,10},{12... | collective-permute-start | bytes 1572872 | tf_op jit(solution)/shard_map/ppermute | solution.py:29
  22.1 4.3 %order.1.measured_ref = f32[6,256,256]{2,1,0:T(8,128)} custom-call(s32[1,1]{1,0:T(1,128)S(6)} %copy.20.counts_ref, bf16[2,256,256]{2,1,0:T(8,128)(2,1)} %constant.193.clone.order_ref, s32[6,256,256]{2,1,0:T(8,128)} %bitcast.2), custom_call_target="tpu_custom_call" | custom-call | flops 402653184 | bytes 3145728 | tf_op jit(solution)/shard_map/order/pallas_call | solution.py:186
  26.4 1.6 %collective-permute-done.3 = f32[2,512,128]{2,1,0:T(8,128)S(1)} collective-permute-done((f32[2,512,128]{2,1,0:T(8,128)S(1)}, f32[2,512,128]{2,1,0:T(8,128)S(1)}, u32[]{:S(2)}, u32[]{:S(2)}) %collective-permute-start.3) | collective-permute-done | bytes 524320 | tf_op jit(solution)/shard_map/ppermute | solution.py:29
  29.6 9.7 %slots.2 = f32[2,512,512]{2,1,0:T(8,128)S(1)} custom-call(s32[6,2]{1,0:T(8,128)S(1)} %copy.8.positions_ref, s32[1,1]{1,0:T(1,128)S(6)} %copy.20.counts_ref, f32[2,512,512]{2,1,0:T(8,128)} %pad_maximum_fusion.padded_ref, f32[2,256,256]{2,1,0:T(8,128)S(1)} %copy-done.1, f32[6,256,256]{2,1,0:T(8,128)S(1)} %copy-done, bf16[2,4,256,256]{3,2,1,0:T(8,128)(2,1)S(1)} %copy-done.2), custom_call_target="tpu_custom_call" | custom-call | flops 4831838208 | bytes 15728640 | tf_op jit(solution)/shard_map/slots/pallas_call | solution.py:200
  39.4 3.8 %collective-permute-start.4 = (f32[2,512,128]{2,1,0:T(8,128)S(1)}, f32[2,512,128]{2,1,0:T(8,128)S(1)}, u32[]{:S(2)}, u32[]{:S(2)}) collective-permute-start(f32[2,512,128]{2,1,0:T(8,128)S(1)} %get-tuple-element.104), channel_id=1, source_target_pairs={{1,0},{2,1},{3,2},{4,3},{5,4},{6,5},{7,6},{9,8},{10,9},{11,10},{12... | collective-permute-start | bytes 1572872 | tf_op jit(solution)/shard_map/ppermute | solution.py:37
  43.2 1.9 %collective-permute-start.5 = (f32[2,512,128]{2,1,0:T(8,128)S(1)}, f32[2,512,128]{2,1,0:T(8,128)S(1)}, u32[]{:S(2)}, u32[]{:S(2)}) collective-permute-start(f32[2,512,128]{2,1,0:T(8,128)S(1)} %get-tuple-element.103), channel_id=1, source_target_pairs={{0,1},{1,2},{2,3},{3,4},{4,5},{5,6},{6,7},{8,9},{9,10},{10,11},{11... | collective-permute-start | bytes 1572872 | tf_op jit(solution)/shard_map/ppermute | solution.py:37
  45.2 4.6 %collective-permute-done.4 = f32[2,512,128]{2,1,0:T(8,128)S(1)} collective-permute-done((f32[2,512,128]{2,1,0:T(8,128)S(1)}, f32[2,512,128]{2,1,0:T(8,128)S(1)}, u32[]{:S(2)}, u32[]{:S(2)}) %collective-permute-start.4) | collective-permute-done | bytes 524320 | tf_op jit(solution)/shard_map/ppermute | solution.py:37
  50.0 3.7 %collective-permute-done.5 = f32[2,512,128]{2,1,0:T(8,128)S(1)} collective-permute-done((f32[2,512,128]{2,1,0:T(8,128)S(1)}, f32[2,512,128]{2,1,0:T(8,128)S(1)}, u32[]{:S(2)}, u32[]{:S(2)}) %collective-permute-start.5) | collective-permute-done | bytes 524320 | tf_op jit(solution)/shard_map/ppermute | solution.py:37
  53.9 7.4 %collective-permute-start.6 = (f32[2,128,256]{2,1,0:T(8,128)S(1)}, f32[2,128,256]{2,1,0:T(8,128)S(1)}, u32[]{:S(2)}, u32[]{:S(2)}) collective-permute-start(f32[2,128,256]{2,1,0:T(8,128)S(1)} %get-tuple-element.110), channel_id=1, source_target_pairs={{8,0},{16,8},{24,16},{9,1},{17,9},{25,17},{10,2},{18,10},{26,18},{... | collective-permute-start | bytes 786440 | tf_op jit(solution)/shard_map/ppermute | solution.py:37
  61.3 1.9 %collective-permute-start.7 = (f32[2,128,256]{2,1,0:T(8,128)S(1)}, f32[2,128,256]{2,1,0:T(8,128)S(1)}, u32[]{:S(2)}, u32[]{:S(2)}) collective-permute-start(f32[2,128,256]{2,1,0:T(8,128)S(1)} %get-tuple-element.109), channel_id=1, source_target_pairs={{0,8},{8,16},{16,24},{1,9},{9,17},{17,25},{2,10},{10,18},{18,26},{... | collective-permute-start | bytes 786440 | tf_op jit(solution)/shard_map/ppermute | solution.py:37
  63.3 1.9 %collective-permute-done.6 = f32[2,128,256]{2,1,0:T(8,128)S(1)} collective-permute-done((f32[2,128,256]{2,1,0:T(8,128)S(1)}, f32[2,128,256]{2,1,0:T(8,128)S(1)}, u32[]{:S(2)}, u32[]{:S(2)}) %collective-permute-start.6) | collective-permute-done | bytes 262176 | tf_op jit(solution)/shard_map/ppermute | solution.py:37
  65.2 7.7 %collective-permute-done.7 = f32[2,128,256]{2,1,0:T(8,128)S(1)} collective-permute-done((f32[2,128,256]{2,1,0:T(8,128)S(1)}, f32[2,128,256]{2,1,0:T(8,128)S(1)}, u32[]{:S(2)}, u32[]{:S(2)}) %collective-permute-start.7) | collective-permute-done | bytes 262176 | tf_op jit(solution)/shard_map/ppermute | solution.py:37
  73.1 1.9 %collective-permute-start.8 = (f32[2,128,256]{2,1,0:T(8,128)S(1)}, f32[2,128,256]{2,1,0:T(8,128)S(1)}, u32[]{:S(2)}, u32[]{:S(2)}) collective-permute-start(f32[2,128,256]{2,1,0:T(8,128)S(1)} %get-tuple-element.113), channel_id=1, source_target_pairs={{0,8},{8,16},{16,24},{1,9},{9,17},{17,25},{2,10},{10,18},{18,26},{... | collective-permute-start | bytes 786440 | tf_op jit(solution)/shard_map/ppermute | solution.py:26
  75.0 4.8 %collective-permute-start.9 = (f32[2,128,256]{2,1,0:T(8,128)S(1)}, f32[2,128,256]{2,1,0:T(8,128)S(1)}, u32[]{:S(2)}, u32[]{:S(2)}) collective-permute-start(f32[2,128,256]{2,1,0:T(8,128)S(1)} %get-tuple-element.114), channel_id=1, source_target_pairs={{8,0},{16,8},{24,16},{9,1},{17,9},{25,17},{10,2},{18,10},{26,18},{... | collective-permute-start | bytes 786440 | tf_op jit(solution)/shard_map/ppermute | solution.py:29
  79.8 5.2 %collective-permute-done.8 = f32[2,128,256]{2,1,0:T(8,128)S(1)} collective-permute-done((f32[2,128,256]{2,1,0:T(8,128)S(1)}, f32[2,128,256]{2,1,0:T(8,128)S(1)}, u32[]{:S(2)}, u32[]{:S(2)}) %collective-permute-start.8) | collective-permute-done | bytes 262176 | tf_op jit(solution)/shard_map/ppermute | solution.py:26
  85.2 1.9 %collective-permute-start.10 = (f32[2,512,128]{2,1,0:T(8,128)S(1)}, f32[2,512,128]{2,1,0:T(8,128)S(1)}, u32[]{:S(2)}, u32[]{:S(2)}) collective-permute-start(f32[2,512,128]{2,1,0:T(8,128)S(1)} %get-tuple-element.107), channel_id=1, source_target_pairs={{0,1},{1,2},{2,3},{3,4},{4,5},{5,6},{6,7},{8,9},{9,10},{10,11},{11... | collective-permute-start | bytes 1572872 | tf_op jit(solution)/shard_map/ppermute | solution.py:26
  87.1 3.6 %collective-permute-start.11 = (f32[2,512,128]{2,1,0:T(8,128)S(1)}, f32[2,512,128]{2,1,0:T(8,128)S(1)}, u32[]{:S(2)}, u32[]{:S(2)}) collective-permute-start(f32[2,512,128]{2,1,0:T(8,128)S(1)} %get-tuple-element.108), channel_id=1, source_target_pairs={{1,0},{2,1},{3,2},{4,3},{5,4},{6,5},{7,6},{9,8},{10,9},{11,10},{12... | collective-permute-start | bytes 1572872 | tf_op jit(solution)/shard_map/ppermute | solution.py:29
  90.8 4.9 %collective-permute-done.10 = f32[2,512,128]{2,1,0:T(8,128)S(1)} collective-permute-done((f32[2,512,128]{2,1,0:T(8,128)S(1)}, f32[2,512,128]{2,1,0:T(8,128)S(1)}, u32[]{:S(2)}, u32[]{:S(2)}) %collective-permute-start.10) | collective-permute-done | bytes 524320 | tf_op jit(solution)/shard_map/ppermute | solution.py:26
  95.7 1.8 %collective-permute-done.11 = f32[2,512,128]{2,1,0:T(8,128)S(1)} collective-permute-done((f32[2,512,128]{2,1,0:T(8,128)S(1)}, f32[2,512,128]{2,1,0:T(8,128)S(1)}, u32[]{:S(2)}, u32[]{:S(2)}) %collective-permute-start.11) | collective-permute-done | bytes 524320 | tf_op jit(solution)/shard_map/ppermute | solution.py:29
  99.0 9.7 %slots.3 = f32[2,512,512]{2,1,0:T(8,128)S(1)} custom-call(s32[6,2]{1,0:T(8,128)S(1)} %copy.8.positions_ref, s32[1,1]{1,0:T(1,128)S(6)} %copy.20.counts_ref, f32[2,512,512]{2,1,0:T(8,128)} %pad_maximum_fusion.1.padded_ref, f32[2,256,256]{2,1,0:T(8,128)S(1)} %copy-done.1, f32[6,256,256]{2,1,0:T(8,128)S(1)} %copy-done, bf16[2,4,256,256]{3,2,1,0:T(8,128)(2,1)S(1)} %copy-done.2), custom_call_target="tpu_custom_call" | custom-call | flops 4831838208 | bytes 15728640 | tf_op jit(solution)/shard_map/slots/pallas_call | solution.py:200
  108.8 3.8 %collective-permute-start.12 = (f32[2,512,128]{2,1,0:T(8,128)S(1)}, f32[2,512,128]{2,1,0:T(8,128)S(1)}, u32[]{:S(2)}, u32[]{:S(2)}) collective-permute-start(f32[2,512,128]{2,1,0:T(8,128)S(1)} %get-tuple-element.102), channel_id=1, source_target_pairs={{1,0},{2,1},{3,2},{4,3},{5,4},{6,5},{7,6},{9,8},{10,9},{11,10},{12... | collective-permute-start | bytes 1572872 | tf_op jit(solution)/shard_map/ppermute | solution.py:37
  112.6 1.9 %collective-permute-start.13 = (f32[2,512,128]{2,1,0:T(8,128)S(1)}, f32[2,512,128]{2,1,0:T(8,128)S(1)}, u32[]{:S(2)}, u32[]{:S(2)}) collective-permute-start(f32[2,512,128]{2,1,0:T(8,128)S(1)} %get-tuple-element.101), channel_id=1, source_target_pairs={{0,1},{1,2},{2,3},{3,4},{4,5},{5,6},{6,7},{8,9},{9,10},{10,11},{11... | collective-permute-start | bytes 1572872 | tf_op jit(solution)/shard_map/ppermute | solution.py:37
  114.7 4.6 %collective-permute-done.12 = f32[2,512,128]{2,1,0:T(8,128)S(1)} collective-permute-done((f32[2,512,128]{2,1,0:T(8,128)S(1)}, f32[2,512,128]{2,1,0:T(8,128)S(1)}, u32[]{:S(2)}, u32[]{:S(2)}) %collective-permute-start.12) | collective-permute-done | bytes 524320 | tf_op jit(solution)/shard_map/ppermute | solution.py:37
  119.4 3.7 %collective-permute-done.13 = f32[2,512,128]{2,1,0:T(8,128)S(1)} collective-permute-done((f32[2,512,128]{2,1,0:T(8,128)S(1)}, f32[2,512,128]{2,1,0:T(8,128)S(1)}, u32[]{:S(2)}, u32[]{:S(2)}) %collective-permute-start.13) | collective-permute-done | bytes 524320 | tf_op jit(solution)/shard_map/ppermute | solution.py:37
  123.3 7.2 %collective-permute-start.14 = (f32[2,128,256]{2,1,0:T(8,128)S(1)}, f32[2,128,256]{2,1,0:T(8,128)S(1)}, u32[]{:S(2)}, u32[]{:S(2)}) collective-permute-start(f32[2,128,256]{2,1,0:T(8,128)S(1)} %get-tuple-element.106), channel_id=1, source_target_pairs={{8,0},{16,8},{24,16},{9,1},{17,9},{25,17},{10,2},{18,10},{26,18},{... | collective-permute-start | bytes 786440 | tf_op jit(solution)/shard_map/ppermute | solution.py:37
  130.5 1.9 %collective-permute-start.15 = (f32[2,128,256]{2,1,0:T(8,128)S(1)}, f32[2,128,256]{2,1,0:T(8,128)S(1)}, u32[]{:S(2)}, u32[]{:S(2)}) collective-permute-start(f32[2,128,256]{2,1,0:T(8,128)S(1)} %get-tuple-element.105), channel_id=1, source_target_pairs={{0,8},{8,16},{16,24},{1,9},{9,17},{17,25},{2,10},{10,18},{18,26},{... | collective-permute-start | bytes 786440 | tf_op jit(solution)/shard_map/ppermute | solution.py:37
  132.5 4.7 %collective-permute-done.14 = f32[2,128,256]{2,1,0:T(8,128)S(1)} collective-permute-done((f32[2,128,256]{2,1,0:T(8,128)S(1)}, f32[2,128,256]{2,1,0:T(8,128)S(1)}, u32[]{:S(2)}, u32[]{:S(2)}) %collective-permute-start.14) | collective-permute-done | bytes 262176 | tf_op jit(solution)/shard_map/ppermute | solution.py:37
  137.2 6.3 %collective-permute-done.15 = f32[2,128,256]{2,1,0:T(8,128)S(1)} collective-permute-done((f32[2,128,256]{2,1,0:T(8,128)S(1)}, f32[2,128,256]{2,1,0:T(8,128)S(1)}, u32[]{:S(2)}, u32[]{:S(2)}) %collective-permute-start.15) | collective-permute-done | bytes 262176 | tf_op jit(solution)/shard_map/ppermute | solution.py:37
  (42 shorter events, 9.2 us)
Async XLA Ops:
  1.1 12.0 %collective-permute-start = (f32[2,128,256]{2,1,0:T(8,128)S(1)}, f32[2,128,256]{2,1,0:T(8,128)S(1)}, u32[]{:S(2)}, u32[]{:S(2)}) collective-permute-start(f32[2,128,256]{2,1,0:T(8,128)S(1)} %get-tuple-element.116), channel_id=1, source_target_pairs={{0,8},{8,16},{16,24},{1,9},{9,17},{17,25},{2,10},{10,18},{18,26},{... | collective-permute-start | bytes 786440 | tf_op jit(solution)/shard_map/ppermute | solution.py:26
  4.5 17.5 %copy-start.4 = (s32[1,1,6,2]{2,3,1,0:T(2,128)S(1)}, s32[1,1,6,2]{2,3,1,0:T(2,128)}, u32[]{:S(2)}) copy-start(s32[1,1,6,2]{2,3,1,0:T(2,128)} %param.25) | copy-start | bytes 148
  4.5 11.1 %collective-permute-start.1 = (f32[2,128,256]{2,1,0:T(8,128)S(1)}, f32[2,128,256]{2,1,0:T(8,128)S(1)}, u32[]{:S(2)}, u32[]{:S(2)}) collective-permute-start(f32[2,128,256]{2,1,0:T(8,128)S(1)} %get-tuple-element.115), channel_id=1, source_target_pairs={{8,0},{16,8},{24,16},{9,1},{17,9},{25,17},{10,2},{18,10},{26,18},{... | collective-permute-start | bytes 786440 | tf_op jit(solution)/shard_map/ppermute | solution.py:29
  15.7 10.6 %collective-permute-start.2 = (f32[2,512,128]{2,1,0:T(8,128)S(1)}, f32[2,512,128]{2,1,0:T(8,128)S(1)}, u32[]{:S(2)}, u32[]{:S(2)}) collective-permute-start(f32[2,512,128]{2,1,0:T(8,128)S(1)} %get-tuple-element.111), channel_id=1, source_target_pairs={{0,1},{1,2},{2,3},{3,4},{4,5},{5,6},{6,7},{8,9},{9,10},{10,11},{11... | collective-permute-start | bytes 1572872 | tf_op jit(solution)/shard_map/ppermute | solution.py:26
  17.7 10.3 %collective-permute-start.3 = (f32[2,512,128]{2,1,0:T(8,128)S(1)}, f32[2,512,128]{2,1,0:T(8,128)S(1)}, u32[]{:S(2)}, u32[]{:S(2)}) collective-permute-start(f32[2,512,128]{2,1,0:T(8,128)S(1)} %get-tuple-element.112), channel_id=1, source_target_pairs={{1,0},{2,1},{3,2},{4,3},{5,4},{6,5},{7,6},{9,8},{10,9},{11,10},{12... | collective-permute-start | bytes 1572872 | tf_op jit(solution)/shard_map/ppermute | solution.py:29
  26.3 3.2 %copy-start = (f32[6,256,256]{2,1,0:T(8,128)S(1)}, f32[6,256,256]{2,1,0:T(8,128)}, u32[]{:S(2)}) copy-start(f32[6,256,256]{2,1,0:T(8,128)} %order.1.measured_ref) | copy-start | bytes 4718596
  26.3 3.2 %copy-start.1 = (f32[2,256,256]{2,1,0:T(8,128)S(1)}, f32[2,256,256]{2,1,0:T(8,128)}, u32[]{:S(2)}) copy-start(f32[2,256,256]{2,1,0:T(8,128)} %probe_ref.3) | copy-start | bytes 1572868
  26.3 3.2 %copy-start.2 = (bf16[2,4,256,256]{3,2,1,0:T(8,128)(2,1)S(1)}, bf16[2,4,256,256]{3,2,1,0:T(8,128)(2,1)}, u32[]{:S(2)}) copy-start(bf16[2,4,256,256]{3,2,1,0:T(8,128)(2,1)} %constant.192.clone.table_ref) | copy-start | bytes 3145732
  39.4 10.5 %collective-permute-start.4 = (f32[2,512,128]{2,1,0:T(8,128)S(1)}, f32[2,512,128]{2,1,0:T(8,128)S(1)}, u32[]{:S(2)}, u32[]{:S(2)}) collective-permute-start(f32[2,512,128]{2,1,0:T(8,128)S(1)} %get-tuple-element.104), channel_id=1, source_target_pairs={{1,0},{2,1},{3,2},{4,3},{5,4},{6,5},{7,6},{9,8},{10,9},{11,10},{12... | collective-permute-start | bytes 1572872 | tf_op jit(solution)/shard_map/ppermute | solution.py:37
  43.2 10.5 %collective-permute-start.5 = (f32[2,512,128]{2,1,0:T(8,128)S(1)}, f32[2,512,128]{2,1,0:T(8,128)S(1)}, u32[]{:S(2)}, u32[]{:S(2)}) collective-permute-start(f32[2,512,128]{2,1,0:T(8,128)S(1)} %get-tuple-element.103), channel_id=1, source_target_pairs={{0,1},{1,2},{2,3},{3,4},{4,5},{5,6},{6,7},{8,9},{9,10},{10,11},{11... | collective-permute-start | bytes 1572872 | tf_op jit(solution)/shard_map/ppermute | solution.py:37
  53.8 19.2 %copy-start.3 = (f32[2,256,256]{2,1,0:T(8,128)S(1)}, f32[2,256,256]{2,1,0:T(8,128)}, u32[]{:S(2)}) copy-start(f32[2,256,256]{2,1,0:T(8,128)} %param.23) | copy-start | bytes 1572868
  53.9 11.3 %collective-permute-start.6 = (f32[2,128,256]{2,1,0:T(8,128)S(1)}, f32[2,128,256]{2,1,0:T(8,128)S(1)}, u32[]{:S(2)}, u32[]{:S(2)}) collective-permute-start(f32[2,128,256]{2,1,0:T(8,128)S(1)} %get-tuple-element.110), channel_id=1, source_target_pairs={{8,0},{16,8},{24,16},{9,1},{17,9},{25,17},{10,2},{18,10},{26,18},{... | collective-permute-start | bytes 786440 | tf_op jit(solution)/shard_map/ppermute | solution.py:37
  61.3 11.6 %collective-permute-start.7 = (f32[2,128,256]{2,1,0:T(8,128)S(1)}, f32[2,128,256]{2,1,0:T(8,128)S(1)}, u32[]{:S(2)}, u32[]{:S(2)}) collective-permute-start(f32[2,128,256]{2,1,0:T(8,128)S(1)} %get-tuple-element.109), channel_id=1, source_target_pairs={{0,8},{8,16},{16,24},{1,9},{9,17},{17,25},{2,10},{10,18},{18,26},{... | collective-permute-start | bytes 786440 | tf_op jit(solution)/shard_map/ppermute | solution.py:37
  73.1 12.0 %collective-permute-start.8 = (f32[2,128,256]{2,1,0:T(8,128)S(1)}, f32[2,128,256]{2,1,0:T(8,128)S(1)}, u32[]{:S(2)}, u32[]{:S(2)}) collective-permute-start(f32[2,128,256]{2,1,0:T(8,128)S(1)} %get-tuple-element.113), channel_id=1, source_target_pairs={{0,8},{8,16},{16,24},{1,9},{9,17},{17,25},{2,10},{10,18},{18,26},{... | collective-permute-start | bytes 786440 | tf_op jit(solution)/shard_map/ppermute | solution.py:26
  75.0 10.0 %collective-permute-start.9 = (f32[2,128,256]{2,1,0:T(8,128)S(1)}, f32[2,128,256]{2,1,0:T(8,128)S(1)}, u32[]{:S(2)}, u32[]{:S(2)}) collective-permute-start(f32[2,128,256]{2,1,0:T(8,128)S(1)} %get-tuple-element.114), channel_id=1, source_target_pairs={{8,0},{16,8},{24,16},{9,1},{17,9},{25,17},{10,2},{18,10},{26,18},{... | collective-permute-start | bytes 786440 | tf_op jit(solution)/shard_map/ppermute | solution.py:29
  85.2 10.5 %collective-permute-start.10 = (f32[2,512,128]{2,1,0:T(8,128)S(1)}, f32[2,512,128]{2,1,0:T(8,128)S(1)}, u32[]{:S(2)}, u32[]{:S(2)}) collective-permute-start(f32[2,512,128]{2,1,0:T(8,128)S(1)} %get-tuple-element.107), channel_id=1, source_target_pairs={{0,1},{1,2},{2,3},{3,4},{4,5},{5,6},{6,7},{8,9},{9,10},{10,11},{11... | collective-permute-start | bytes 1572872 | tf_op jit(solution)/shard_map/ppermute | solution.py:26
  87.1 10.3 %collective-permute-start.11 = (f32[2,512,128]{2,1,0:T(8,128)S(1)}, f32[2,512,128]{2,1,0:T(8,128)S(1)}, u32[]{:S(2)}, u32[]{:S(2)}) collective-permute-start(f32[2,512,128]{2,1,0:T(8,128)S(1)} %get-tuple-element.108), channel_id=1, source_target_pairs={{1,0},{2,1},{3,2},{4,3},{5,4},{6,5},{7,6},{9,8},{10,9},{11,10},{12... | collective-permute-start | bytes 1572872 | tf_op jit(solution)/shard_map/ppermute | solution.py:29
  108.8 10.5 %collective-permute-start.12 = (f32[2,512,128]{2,1,0:T(8,128)S(1)}, f32[2,512,128]{2,1,0:T(8,128)S(1)}, u32[]{:S(2)}, u32[]{:S(2)}) collective-permute-start(f32[2,512,128]{2,1,0:T(8,128)S(1)} %get-tuple-element.102), channel_id=1, source_target_pairs={{1,0},{2,1},{3,2},{4,3},{5,4},{6,5},{7,6},{9,8},{10,9},{11,10},{12... | collective-permute-start | bytes 1572872 | tf_op jit(solution)/shard_map/ppermute | solution.py:37
  112.6 10.5 %collective-permute-start.13 = (f32[2,512,128]{2,1,0:T(8,128)S(1)}, f32[2,512,128]{2,1,0:T(8,128)S(1)}, u32[]{:S(2)}, u32[]{:S(2)}) collective-permute-start(f32[2,512,128]{2,1,0:T(8,128)S(1)} %get-tuple-element.101), channel_id=1, source_target_pairs={{0,1},{1,2},{2,3},{3,4},{4,5},{5,6},{6,7},{8,9},{9,10},{10,11},{11... | collective-permute-start | bytes 1572872 | tf_op jit(solution)/shard_map/ppermute | solution.py:37
  123.3 13.9 %collective-permute-start.14 = (f32[2,128,256]{2,1,0:T(8,128)S(1)}, f32[2,128,256]{2,1,0:T(8,128)S(1)}, u32[]{:S(2)}, u32[]{:S(2)}) collective-permute-start(f32[2,128,256]{2,1,0:T(8,128)S(1)} %get-tuple-element.106), channel_id=1, source_target_pairs={{8,0},{16,8},{24,16},{9,1},{17,9},{25,17},{10,2},{18,10},{26,18},{... | collective-permute-start | bytes 786440 | tf_op jit(solution)/shard_map/ppermute | solution.py:37
  130.5 13.0 %collective-permute-start.15 = (f32[2,128,256]{2,1,0:T(8,128)S(1)}, f32[2,128,256]{2,1,0:T(8,128)S(1)}, u32[]{:S(2)}, u32[]{:S(2)}) collective-permute-start(f32[2,128,256]{2,1,0:T(8,128)S(1)} %get-tuple-element.105), channel_id=1, source_target_pairs={{0,8},{8,16},{16,24},{1,9},{9,17},{17,25},{2,10},{10,18},{18,26},{... | collective-permute-start | bytes 786440 | tf_op jit(solution)/shard_map/ppermute | solution.py:37
where the time goes:
time: 147 us; the launch traced here: 144 us
  waiting for transfers between devices  57.5 us (39%)
  starting transfers between devices  54.5 us (37%)
  Pallas kernels  23.7 us (16%)
  other arithmetic  4.76 us (3%)
  local copies, waits for them, and re-layouts  2.96 us (2%)
    ppermute x8, waiting for transfers between devices, from_behind(): return lax.ppermute(block, axis, route)  37.3 us
    ppermute x8, starting transfers between devices, from_behind(): return lax.ppermute(block, axis, route)  29.9 us
    pallas_call x2, Pallas kernels, slot_terms(): pl.pallas_call(slots_kernel, out_shape=jax.ShapeDtypeStruct(padded.shape,...  19.4 us
    ppermute x4, starting transfers between devices, extended(): lax.ppermute(lax.slice_in_dim(block, 0, width, axis=dim), axis, backward)  15.4 us
    ppermute x4, waiting for transfers between devices, extended(): lax.ppermute(lax.slice_in_dim(block, block.shape[dim] - width, None, axis...  15.3 us
    ppermute x4, starting transfers between devices, extended(): lax.ppermute(lax.slice_in_dim(block, block.shape[dim] - width, None, axis...  9.16 us
    ppermute x4, waiting for transfers between devices, extended(): lax.ppermute(lax.slice_in_dim(block, 0, width, axis=dim), axis, backward)  4.89 us
    pallas_call x1, Pallas kernels, in_order(): pl.pallas_call(order_kernel, out_shape=jax.ShapeDtypeStruct((slots, size,...  4.28 us
  transfers between devices with their start and end apart: 16, of which 14 were waited for; matrix products, arithmetic and copies ran while one was open for 1% of the time, Pallas kernels for 3%

commit v1 on v0

--- a/solution.py
+++ b/solution.py
@@ -16,25 +16,6 @@
 
 step_rate = 0.02
 photon_unit = 0.001
-
-
-def extended(block, sides, width):
-    for axis, dim in sides:
-        count = lax.axis_size(axis)
-        forward = [(i, i + 1) for i in range(count - 1)]
-        backward = [(target, source) for source, target in forward]
-        low = lax.ppermute(
-            lax.slice_in_dim(block, block.shape[dim] - width, None, axis=dim), axis, forward
-        )
-        high = lax.ppermute(lax.slice_in_dim(block, 0, width, axis=dim), axis, backward)
-        block = jnp.concatenate([low, block, high], axis=dim)
-    return block
-
-
-def from_behind(block, axis, distance):
-    devices = range(lax.axis_size(axis))
-    route = [(i - distance, i) for i in devices if i - distance in devices]
-    return lax.ppermute(block, axis, route)
 
 
 def tables(length):
@@ -210,31 +191,244 @@
     )(positions, counts, padded, probe, measured, table)
 
 
+MESH = pl.DeviceIdType.MESH
+
+
+class Around:
+    def __init__(self, send_sems, recv_sems):
+        self.send_sems, self.recv_sems = send_sems, recv_sems
+        self.here, self.device = {}, {}
+        for axis in ("rows", "cols"):
+            count = lax.axis_size(axis)
+            me = lax.axis_index(axis)
+            self.here[axis, -1], self.here[axis, 1] = me > 0, me < count - 1
+            self.device[axis, -1] = {axis: lax.rem(me + count - 1, count)}
+            self.device[axis, 1] = {axis: lax.rem(me + 1, count)}
+
+    def meet(self):
+        barrier = pltpu.get_barrier_semaphore()
+        for side, there in self.here.items():
+
+            @pl.when(there)
+            def _():
+                pl.semaphore_signal(barrier, inc=1, device_id=self.device[side], device_id_type=MESH)
+
+        pl.semaphore_wait(barrier, sum(there.astype(jnp.int32) for there in self.here.values()))
+
+    def copy(self, index, side, source, target):
+        return pltpu.make_async_remote_copy(
+            src_ref=source,
+            dst_ref=target,
+            send_sem=self.send_sems.at[index],
+            recv_sem=self.recv_sems.at[index],
+            device_id=self.device[side],
+            device_id_type=MESH,
+        )
+
+
+def both(first, second):
+    return jnp.logical_and(first, second)
+
+
+def no(flag):
+    return jnp.logical_not(flag)
+
+
+def pad_kernel(field_ref, out_ref, send_sems, recv_sems):
+    m = MARGIN
+    planes, high, wide = field_ref.shape
+    around = Around(send_sems, recv_sems)
+    here = around.here
+    around.meet()
+    row_cuts = {-1: (pl.ds(0, m), pl.ds(m + high, m)), 1: (pl.ds(high - m, m), pl.ds(0, m))}
+    col_cuts = {-1: (pl.ds(0, m), pl.ds(m + wide, m)), 1: (pl.ds(wide - m, m), pl.ds(0, m))}
+    from_cuts = {-1: pl.ds(0, m), 1: pl.ds(m + high, m)}
+    col_from = {-1: pl.ds(m, m), 1: pl.ds(wide, m)}
+    rows, cols, corners = {}, {}, {}
+    index = 0
+    for p in range(planes):
+        for d in (-1, 1):
+            cut, land = row_cuts[d]
+            rows[p, d] = around.copy(
+                index, ("rows", d), field_ref.at[p, cut, :], out_ref.at[p, land, pl.ds(m, wide)]
+            )
+            cut, land = col_cuts[d]
+            cols[p, d] = around.copy(
+                index + 1, ("cols", d), field_ref.at[p, :, cut], out_ref.at[p, pl.ds(m, high), land]
+            )
+            index += 2
+            for v in (-1, 1):
+                corners[p, v, d] = around.copy(
+                    index, ("cols", d), out_ref.at[p, from_cuts[v], col_from[d]], out_ref.at[p, from_cuts[v], land]
+                )
+                index += 1
+    for p in range(planes):
+        for d in (-1, 1):
+            pl.when(here["rows", d])(rows[p, d].start)
+    for p in range(planes):
+        for d in (-1, 1):
+            pl.when(here["cols", d])(cols[p, d].start)
+    out_ref[:, m : m + high, m : m + wide] = field_ref[...]
+    for v in (-1, 1):
+
+        @pl.when(no(here["rows", v]))
+        def _():
+            out_ref[:, from_cuts[v], m : m + wide] = jnp.zeros((planes, m, wide), jnp.float32)
+
+        for d in (-1, 1):
+            land = col_cuts[-d][1]
+
+            @pl.when(no(both(here["rows", v], here["cols", d])))
+            def _():
+                out_ref[:, from_cuts[v], land] = jnp.zeros((planes, m, m), jnp.float32)
+
+    for d in (-1, 1):
+        land = col_cuts[-d][1]
+
+        @pl.when(no(here["cols", d]))
+        def _():
+            out_ref[:, m : m + high, land] = jnp.zeros((planes, high, m), jnp.float32)
+
+    for p in range(planes):
+        for v in (-1, 1):
+            pl.when(here["rows", v])(rows[p, -v].wait_recv)
+            for d in (-1, 1):
+                pl.when(both(here["rows", v], here["cols", d]))(corners[p, v, d].start)
+    for p in range(planes):
+        for d in (-1, 1):
+            pl.when(here["cols", d])(cols[p, -d].wait_recv)
+            for v in (-1, 1):
+                pl.when(both(here["rows", v], here["cols", d]))(corners[p, v, -d].wait_recv)
+    for p in range(planes):
+        for d in (-1, 1):
+            pl.when(here["rows", d])(rows[p, d].wait_send)
+            pl.when(here["cols", d])(cols[p, d].wait_send)
+            for v in (-1, 1):
+                pl.when(both(here["rows", v], here["cols", d]))(corners[p, v, d].wait_send)
+
+
+def step_kernel(last, grad_ref, padded_ref, out_ref, mid_ref, side_ref, band_ref, send_sems, recv_sems):
+    m = MARGIN
+    planes, extent, _ = grad_ref.shape
+    tall = extent // 2
+    wide = extent - 2 * m
+    around = Around(send_sems, recv_sems)
+    here = around.here
+    around.meet()
+    chains = [(p, h) for p in range(planes) for h in (-1, 1)]
+    halves = {-1: pl.ds(0, tall), 1: pl.ds(tall, tall)}
+    own = {-1: pl.ds(m, tall - m), 1: pl.ds(tall, tall - m)}
+    sides, bands, edges = {}, {}, {}
+    index = 0
+    cut = {-1: pl.ds(0, m), 1: pl.ds(extent - m, m)}
+    inner = {-1: pl.ds(m, m), 1: pl.ds(wide, m)}
+    for p, h in chains:
+        for d in (-1, 1):
+            slot = (d + 1) // 2
+            sides[p, h, d] = around.copy(
+                index, ("cols", d), grad_ref.at[p, halves[h], cut[d]], side_ref.at[slot, p, halves[h]]
+            )
+            index += 1
+            if not last:
+                edges[p, h, d] = around.copy(
+                    index, ("cols", d), out_ref.at[p, halves[h], inner[d]], out_ref.at[p, halves[h], cut[-d]]
+                )
+                index += 1
+        if last:
+            goes, lands = cut[h], own[-h]
+        else:
+            goes, lands = halves[h], halves[-h]
+        bands[p, h] = around.copy(index, ("rows", h), mid_ref.at[p, goes], band_ref.at[p, lands])
+        index += 1
+    for p, h in chains:
+        for d in (-1, 1):
+            pl.when(here["cols", d])(sides[p, h, d].start)
+    if not last:
+        for d in (-1, 1):
+
+            @pl.when(no(here["cols", d]))
+            def _():
+                out_ref[:, :, cut[d]] = jnp.zeros((planes, extent, m), jnp.float32)
+
+    for p, h in chains:
+        mid_ref[p, halves[h]] = grad_ref[p, halves[h], m : m + wide]
+        for d in (-1, 1):
+            slot = (1 - d) // 2
+            target = pl.ds(0, m) if d < 0 else pl.ds(wide - m, m)
+
+            @pl.when(here["cols", d])
+            def _():
+                sides[p, h, -d].wait_recv()
+                mid_ref[p, halves[h], target] += side_ref[slot, p, halves[h]]
+
+        pl.when(here["rows", h])(bands[p, h].start)
+    for p, h in chains:
+        whole = own[h] if last else halves[h]
+
+        @pl.when(here["rows", h])
+        def _():
+            bands[p, -h].wait_recv()
+            total = mid_ref[p, whole] + band_ref[p, whole]
+            value = padded_ref[p, whole, m : m + wide] - step_rate * total
+            if last:
+                out_ref[p, pl.ds(own[h].start - m, tall - m)] = value
+            else:
+                out_ref[p, whole, m : m + wide] = value
+
+        @pl.when(no(here["rows", h]))
+        def _():
+            value = padded_ref[p, own[h], m : m + wide] - step_rate * mid_ref[p, own[h]]
+            if last:
+                out_ref[p, pl.ds(own[h].start - m, tall - m)] = value
+            else:
+                out_ref[p, own[h], m : m + wide] = value
+                out_ref[p, cut[h], m : m + wide] = jnp.zeros((m, wide), jnp.float32)
+
+        if not last:
+            for d in (-1, 1):
+                pl.when(here["cols", d])(edges[p, h, d].start)
+    for p, h in chains:
+        for d in (-1, 1):
+            if not last:
+                pl.when(here["cols", d])(edges[p, h, -d].wait_recv)
+                pl.when(here["cols", d])(edges[p, h, d].wait_send)
+            pl.when(here["cols", d])(sides[p, h, d].wait_send)
+        pl.when(here["rows", h])(bands[p, h].wait_send)
+
+
+def exchange(kernel, name, collective_id, shape, scratch, copies, *arrays):
+    return pl.pallas_call(
+        kernel,
+        out_shape=jax.ShapeDtypeStruct(shape, jnp.float32),
+        in_specs=[pl.BlockSpec(memory_space=pltpu.VMEM)] * len(arrays),
+        out_specs=pl.BlockSpec(memory_space=pltpu.VMEM),
+        scratch_shapes=[pltpu.VMEM(s, jnp.float32) for s in scratch]
+        + [pltpu.SemaphoreType.DMA((copies,)), pltpu.SemaphoreType.DMA((copies,))],
+        compiler_params=pltpu.CompilerParams(
+            collective_id=collective_id, has_side_effects=True, vmem_limit_bytes=32 * 1024 * 1024
+        ),
+        name=name,
+    )(*arrays)
+
+
 def on_device(object_field, probe, positions, counts, intensity):
-    tile = object_field.shape[1]
+    planes, high, wide = object_field.shape
     size = probe.shape[1]
     table = jnp.asarray(tables(size))
     order = jnp.asarray(ordering(size))
     positions = positions[0, 0]
     measured = in_order(counts, intensity[0, 0], order)
-    field = object_field
+    tall, broad = high + 2 * MARGIN, wide + 2 * MARGIN
+    outer = (planes, tall, broad)
+    scratch = [(planes, tall, wide), (2, planes, tall, MARGIN), (planes, tall, wide)]
+    padded = exchange(pad_kernel, "pad", 0, outer, [], 8 * planes, object_field)
     for step in range(ITERS):
-        padded = extended(field, (("rows", 1), ("cols", 2)), MARGIN)
         grad = slot_terms(positions, counts, padded, probe, measured, table)
-        low = MARGIN
-        high = MARGIN + tile
-        from_right_side = from_behind(grad[:, :, :low], "cols", -1)
-        from_left_side = from_behind(grad[:, :, high:], "cols", 1)
-        middle = grad[:, :, low:high]
-        middle = middle.at[:, :, tile - low :].add(from_right_side)
-        middle = middle.at[:, :, :low].add(from_left_side)
-        from_below = from_behind(middle[:, :low, :], "rows", -1)
-        from_above = from_behind(middle[:, high:, :], "rows", 1)
-        owned = middle[:, low:high, :]
-        owned = owned.at[:, tile - low :, :].add(from_below)
-        owned = owned.at[:, :low, :].add(from_above)
-        field = field - step_rate * owned
-    return field
+        last = step == ITERS - 1
+        kernel = functools.partial(step_kernel, last)
+        shape = object_field.shape if last else outer
+        padded = exchange(kernel, "step", 1 + step, shape, scratch, 10 * planes, grad, padded)
+    return padded
 
 
 def solution(mesh):

time: 147 us -> 108 us (0.73); the launches traced: 144 us -> 108 us
  Pallas kernels: 23.7 us -> 100 us
  waiting for transfers between devices: 57.5 us -> 0 us
  starting transfers between devices: 54.5 us -> 0 us
  other arithmetic: 4.76 us -> 0 us
  local copies, waits for them, and re-layouts: 2.96 us -> 7.43 us
    pallas_call x0 -> x3, Pallas kernels: none -> 85.3 us  [exchange(): pl.pallas_call(kernel, out_shape=jax.ShapeDtypeStruct(shape, jnp.float32)...]
    ppermute x16 -> x0, waiting for transfers between devices: 57.5 us -> none  [the longest x8 37.3 us: from_behind(): return lax.ppermute(block, axis, route)]
    ppermute x16 -> x0, starting transfers between devices: 54.5 us -> none  [the longest x8 29.9 us: from_behind(): return lax.ppermute(block, axis, route)]
    pallas_call x2, Pallas kernels: 19.4 us -> 11.5 us  [slot_terms(): pl.pallas_call(slots_kernel, out_shape=jax.ShapeDtypeStruct(padded.shape,...]
    unnamed x12 -> x17, local copies, waits for them, and re-layouts: 1.12 us -> 6.66 us
    concatenate x3 -> x0, other arithmetic: 3.23 us -> none  [extended(): block = jnp.concatenate([low, block, high], axis=dim)]
    slice x12 -> x0, local copies, waits for them, and re-layouts: 1.73 us -> none  [the longest x1 1.06 us: extended(): lax.slice_in_dim(block, 0, width, axis=dim)]
  transfers between devices with their start and end apart: 16 -> 0, of which waited for: 14 -> 0; matrix products, arithmetic and copies ran while one was open for 1% -> 0% of each run, Pallas kernels for 3% -> 0%
where the time goes in v1:
time: 108 us
  Pallas kernels  100 us (93%)
  local copies, waits for them, and re-layouts  7.43 us (7%)
    pallas_call x3, Pallas kernels, exchange(): pl.pallas_call(kernel, out_shape=jax.ShapeDtypeStruct(shape, jnp.float32)...  85.3 us
    pallas_call x2, Pallas kernels, slot_terms(): pl.pallas_call(slots_kernel, out_shape=jax.ShapeDtypeStruct(padded.shape,...  11.5 us
    unnamed x17, local copies, waits for them, and re-layouts  6.66 us
    pallas_call x1, Pallas kernels, in_order(): pl.pallas_call(order_kernel, out_shape=jax.ShapeDtypeStruct((slots, size,...  3.54 us

profile of v1, /device:TPU:12, one launch (start us, length us, event | category | flops | bytes accessed | tf_op | source)
XLA Modules:
  0.0 108.5 jit_solution(15747493999684766674)
XLA Ops:
  0.0 0.0 copy-start.5
  0.7 0.8 copy.9.positions_ref
  1.5 0.0 copy-start.7
  1.5 3.5 %order.1.measured_ref = f32[6,256,256]{2,1,0:T(8,128)} custom-call(s32[1,1]{1,0:T(1,128)S(6)} %copy.11.counts_ref, bf16[2,256,256]{2,1,0:T(8,128)(2,1)} %constant.5.clone.order_ref, s32[6,256,256]{2,1,0:T(8,128)} %bitcast.2), custom_call_target="tpu_custom_call" | custom-call | flops 402653184 | bytes 3145728 | tf_op jit(solution)/shard_map/order/pallas_call | solution.py:167
  5.0 0.0 copy-done.5
  5.0 0.0 copy-start.4
  5.0 0.0 copy-start.6
  5.0 18.2 %pad.1.padded_ref = f32[2,512,512]{2,1,0:T(8,128)S(1)} custom-call(f32[2,256,256]{2,1,0:T(8,128)S(1)} %copy-done.5), custom_call_target="tpu_custom_call" | custom-call | tf_op jit(solution)/shard_map/pad/pallas_call | solution.py:400
  23.3 0.0 copy-start
  23.3 1.3 %copy-done = f32[2,512,512]{2,1,0:T(8,128)} copy-done((f32[2,512,512]{2,1,0:T(8,128)}, f32[2,512,512]{2,1,0:T(8,128)S(1)}, u32[]{:S(2)}) %copy-start) | copy-done | bytes 2097176
  24.6 0.0 copy-done.7
  24.6 0.0 copy-done.4
  24.6 0.0 copy-done.6
  24.6 5.7 %slots.2.grad_ref = f32[2,512,512]{2,1,0:T(8,128)S(1)} custom-call(s32[6,2]{1,0:T(8,128)S(1)} %copy.9.positions_ref, s32[1,1]{1,0:T(1,128)S(6)} %copy.11.counts_ref, f32[2,512,512]{2,1,0:T(8,128)} %copy-done, f32[2,256,256]{2,1,0:T(8,128)S(1)} %copy-done.6, f32[6,256,256]{2,1,0:T(8,128)S(1)} %copy-done.4, bf16[2,4,256,256]{3,2,1,0:T(8,128)(2,1)S(1)} %copy-done.7), custom_call_target="tpu_custom_call" | custom-call | flops 4831838208 | bytes 15728640 | tf_op jit(solution)/shard_map/slots/pallas_call | solution.py:181
  30.4 0.0 copy-start.1
  30.4 1.6 %copy-done.1 = f32[2,512,512]{2,1,0:T(8,128)S(1)} copy-done((f32[2,512,512]{2,1,0:T(8,128)S(1)}, f32[2,512,512]{2,1,0:T(8,128)}, u32[]{:S(2)}) %copy-start.1) | copy-done | bytes 2097176
  31.9 41.9 %step.2.padded_ref = f32[2,512,512]{2,1,0:T(8,128)S(1)} custom-call(f32[2,512,512]{2,1,0:T(8,128)S(1)} %slots.2.grad_ref, f32[2,512,512]{2,1,0:T(8,128)S(1)} %copy-done.1), custom_call_target="tpu_custom_call" | custom-call | tf_op jit(solution)/shard_map/step/pallas_call | solution.py:400
  73.8 0.0 copy-start.2
  73.8 1.3 %copy-done.2 = f32[2,512,512]{2,1,0:T(8,128)} copy-done((f32[2,512,512]{2,1,0:T(8,128)}, f32[2,512,512]{2,1,0:T(8,128)S(1)}, u32[]{:S(2)}) %copy-start.2) | copy-done | bytes 2097176
  75.2 5.7 %slots.3.grad_ref = f32[2,512,512]{2,1,0:T(8,128)S(1)} custom-call(s32[6,2]{1,0:T(8,128)S(1)} %copy.9.positions_ref, s32[1,1]{1,0:T(1,128)S(6)} %copy.11.counts_ref, f32[2,512,512]{2,1,0:T(8,128)} %copy-done.2, f32[2,256,256]{2,1,0:T(8,128)S(1)} %copy-done.6, f32[6,256,256]{2,1,0:T(8,128)S(1)} %copy-done.4, bf16[2,4,256,256]{3,2,1,0:T(8,128)(2,1)S(1)} %copy-done.7), custom_call_target="tpu_custom_call" | custom-call | flops 4831838208 | bytes 15728640 | tf_op jit(solution)/shard_map/slots/pallas_call | solution.py:181
  80.9 0.0 copy-start.3
  80.9 1.6 %copy-done.3 = f32[2,512,512]{2,1,0:T(8,128)S(1)} copy-done((f32[2,512,512]{2,1,0:T(8,128)S(1)}, f32[2,512,512]{2,1,0:T(8,128)}, u32[]{:S(2)}) %copy-start.3) | copy-done | bytes 2097176
  82.5 25.2 %step.3 = f32[2,256,256]{2,1,0:T(8,128)S(1)} custom-call(f32[2,512,512]{2,1,0:T(8,128)S(1)} %slots.3.grad_ref, f32[2,512,512]{2,1,0:T(8,128)S(1)} %copy-done.3), custom_call_target="tpu_custom_call" | custom-call | tf_op jit(solution)/shard_map/step/pallas_call | solution.py:400
  107.7 0.8 copy.12
Async XLA Ops:
  0.0 5.0 %copy-start.5 = (f32[2,256,256]{2,1,0:T(8,128)S(1)}, f32[2,256,256]{2,1,0:T(8,128)}, u32[]{:S(2)}) copy-start(f32[2,256,256]{2,1,0:T(8,128)} %field_ref.1) | copy-start | bytes 1572868
  1.5 23.1 %copy-start.7 = (bf16[2,4,256,256]{3,2,1,0:T(8,128)(2,1)S(1)}, bf16[2,4,256,256]{3,2,1,0:T(8,128)(2,1)}, u32[]{:S(2)}) copy-start(bf16[2,4,256,256]{3,2,1,0:T(8,128)(2,1)} %constant.4.clone.table_ref) | copy-start | bytes 3145732
  5.0 19.6 %copy-start.4 = (f32[6,256,256]{2,1,0:T(8,128)S(1)}, f32[6,256,256]{2,1,0:T(8,128)}, u32[]{:S(2)}) copy-start(f32[6,256,256]{2,1,0:T(8,128)} %order.1.measured_ref) | copy-start | bytes 4718596
  5.0 19.6 %copy-start.6 = (f32[2,256,256]{2,1,0:T(8,128)S(1)}, f32[2,256,256]{2,1,0:T(8,128)}, u32[]{:S(2)}) copy-start(f32[2,256,256]{2,1,0:T(8,128)} %probe_ref.3) | copy-start | bytes 1572868
  23.3 1.3 %copy-start = (f32[2,512,512]{2,1,0:T(8,128)}, f32[2,512,512]{2,1,0:T(8,128)S(1)}, u32[]{:S(2)}) copy-start(f32[2,512,512]{2,1,0:T(8,128)S(1)} %pad.1.padded_ref) | copy-start | bytes 6291460
  30.4 1.6 %copy-start.1 = (f32[2,512,512]{2,1,0:T(8,128)S(1)}, f32[2,512,512]{2,1,0:T(8,128)}, u32[]{:S(2)}) copy-start(f32[2,512,512]{2,1,0:T(8,128)} %copy-done) | copy-start | bytes 6291460
  73.8 1.3 %copy-start.2 = (f32[2,512,512]{2,1,0:T(8,128)}, f32[2,512,512]{2,1,0:T(8,128)S(1)}, u32[]{:S(2)}) copy-start(f32[2,512,512]{2,1,0:T(8,128)S(1)} %step.2.padded_ref) | copy-start | bytes 6291460
  80.9 1.6 %copy-start.3 = (f32[2,512,512]{2,1,0:T(8,128)S(1)}, f32[2,512,512]{2,1,0:T(8,128)}, u32[]{:S(2)}) copy-start(f32[2,512,512]{2,1,0:T(8,128)} %copy-done.2) | copy-start | bytes 6291460

commit v2 on v1

--- a/solution.py
+++ b/solution.py
@@ -172,6 +172,7 @@
         cost_estimate=pl.CostEstimate(
             flops=slots * 4 * size**3, bytes_accessed=slots * 8 * size**2, transcendentals=0
         ),
+        compiler_params=pltpu.CompilerParams(vmem_limit_bytes=12 * 1024 * 1024),
         name="order",
     )(counts, order, intensity)
 
@@ -186,7 +187,7 @@
         cost_estimate=pl.CostEstimate(
             flops=slots * 48 * size**3, bytes_accessed=slots * 40 * size**2, transcendentals=0
         ),
-        compiler_params=pltpu.CompilerParams(vmem_limit_bytes=48 * 1024 * 1024),
+        compiler_params=pltpu.CompilerParams(vmem_limit_bytes=20 * 1024 * 1024),
         name="slots",
     )(positions, counts, padded, probe, measured, table)
 
@@ -405,7 +406,7 @@
         scratch_shapes=[pltpu.VMEM(s, jnp.float32) for s in scratch]
         + [pltpu.SemaphoreType.DMA((copies,)), pltpu.SemaphoreType.DMA((copies,))],
         compiler_params=pltpu.CompilerParams(
-            collective_id=collective_id, has_side_effects=True, vmem_limit_bytes=32 * 1024 * 1024
+            collective_id=collective_id, has_side_effects=True, vmem_limit_bytes=12 * 1024 * 1024
         ),
         name=name,
     )(*arrays)

time: 108 us -> 98.8 us (0.915); the launches traced: 108 us -> 98.2 us
  Pallas kernels: 100 us -> 93.5 us
  local copies, waits for them, and re-layouts: 7.43 us -> 3.94 us
    pallas_call x3, Pallas kernels: 85.3 us -> 70 us  [exchange(): pl.pallas_call(kernel, out_shape=jax.ShapeDtypeStruct(shape, jnp.float32)...]
    pallas_call x2, Pallas kernels: 11.5 us -> 21.4 us  [slot_terms(): pl.pallas_call(slots_kernel, out_shape=jax.ShapeDtypeStruct(padded.shape,...]
    unnamed x17 -> x11, local copies, waits for them, and re-layouts: 6.66 us -> 3.17 us
    pallas_call x1, Pallas kernels: 3.54 us -> 2.04 us  [in_order(): pl.pallas_call(order_kernel, out_shape=jax.ShapeDtypeStruct((slots, size,...]
where the time goes in v2:
time: 98.8 us; the launch traced here: 98.2 us
  Pallas kernels  93.5 us (95%)
  local copies, waits for them, and re-layouts  3.94 us (4%)
    pallas_call x3, Pallas kernels, exchange(): pl.pallas_call(kernel, out_shape=jax.ShapeDtypeStruct(shape, jnp.float32)...  70 us
    pallas_call x2, Pallas kernels, slot_terms(): pl.pallas_call(slots_kernel, out_shape=jax.ShapeDtypeStruct(padded.shape,...  21.4 us
    unnamed x11, local copies, waits for them, and re-layouts  3.17 us
    pallas_call x1, Pallas kernels, in_order(): pl.pallas_call(order_kernel, out_shape=jax.ShapeDtypeStruct((slots, size,...  2.04 us

profile of v2, /device:TPU:12, one launch (start us, length us, event | category | flops | bytes accessed | tf_op | source)
XLA Modules:
  0.0 98.2 jit_solution(7847577501615902415)
XLA Ops:
  0.7 0.8 copy.9.positions_ref
  1.4 0.0 copy-start
  1.4 1.4 %copy-done = s32[1,1,6,256,256]{4,3,2,1,0:T(8,128)S(1)} copy-done((s32[1,1,6,256,256]{4,3,2,1,0:T(8,128)S(1)}, s32[1,1,6,256,256]{4,3,2,1,0:T(8,128)}, u32[]{:S(2)}) %copy-start) | copy-done | bytes 1572888
  2.8 0.0 copy-start.2
  2.8 0.9 copy-done.2
  3.8 0.0 copy-start.1
  3.8 2.0 %order.1.measured_ref = f32[6,256,256]{2,1,0:T(8,128)S(1)} custom-call(s32[1,1]{1,0:T(1,128)S(6)} %copy.11.counts_ref, bf16[2,256,256]{2,1,0:T(8,128)(2,1)S(1)} %copy-done.2, s32[6,256,256]{2,1,0:T(8,128)S(1)} %bitcast.2), custom_call_target="tpu_custom_call" | custom-call | flops 402653184 | bytes 3145728 | tf_op jit(solution)/shard_map/order/pallas_call | solution.py:167
  5.8 0.0 copy-done.1
  5.8 0.0 copy-start.3
  5.9 0.0 copy-start.4
  5.9 18.1 %pad.1.padded_ref = f32[2,512,512]{2,1,0:T(8,128)S(1)} custom-call(f32[2,256,256]{2,1,0:T(8,128)S(1)} %copy-done.1), custom_call_target="tpu_custom_call" | custom-call | tf_op jit(solution)/shard_map/pad/pallas_call | solution.py:401
  24.0 0.0 copy-done.3
  24.0 0.0 copy-done.4
  24.0 10.7 %slots.2.grad_ref = f32[2,512,512]{2,1,0:T(8,128)S(1)} custom-call(s32[6,2]{1,0:T(8,128)S(1)} %copy.9.positions_ref, s32[1,1]{1,0:T(1,128)S(6)} %copy.11.counts_ref, f32[2,512,512]{2,1,0:T(8,128)S(1)} %pad.1.padded_ref, f32[2,256,256]{2,1,0:T(8,128)S(1)} %copy-done.3, f32[6,256,256]{2,1,0:T(8,128)S(1)} %order.1.measured_ref, ...), custom_call_target="tpu_custom_call" | custom-call | flops 4831838208 | bytes 15728640 | tf_op jit(solution)/shard_map/slots/pallas_call | solution.py:182
  34.7 33.8 %step.2.padded_ref = f32[2,512,512]{2,1,0:T(8,128)S(1)} custom-call(f32[2,512,512]{2,1,0:T(8,128)S(1)} %slots.2.grad_ref, f32[2,512,512]{2,1,0:T(8,128)S(1)} %pad.1.padded_ref), custom_call_target="tpu_custom_call" | custom-call | tf_op jit(solution)/shard_map/step/pallas_call | solution.py:401
  68.5 10.7 %slots.3.grad_ref = f32[2,512,512]{2,1,0:T(8,128)S(1)} custom-call(s32[6,2]{1,0:T(8,128)S(1)} %copy.9.positions_ref, s32[1,1]{1,0:T(1,128)S(6)} %copy.11.counts_ref, f32[2,512,512]{2,1,0:T(8,128)S(1)} %step.2.padded_ref, f32[2,256,256]{2,1,0:T(8,128)S(1)} %copy-done.3, f32[6,256,256]{2,1,0:T(8,128)S(1)} %order.1.measured_ref, ...), custom_call_target="tpu_custom_call" | custom-call | flops 4831838208 | bytes 15728640 | tf_op jit(solution)/shard_map/slots/pallas_call | solution.py:182
  79.2 18.2 %step.3 = f32[2,256,256]{2,1,0:T(8,128)S(1)} custom-call(f32[2,512,512]{2,1,0:T(8,128)S(1)} %slots.3.grad_ref, f32[2,512,512]{2,1,0:T(8,128)S(1)} %step.2.padded_ref), custom_call_target="tpu_custom_call" | custom-call | tf_op jit(solution)/shard_map/step/pallas_call | solution.py:401
  97.4 0.8 copy.12
Async XLA Ops:
  1.4 1.4 %copy-start = (s32[1,1,6,256,256]{4,3,2,1,0:T(8,128)S(1)}, s32[1,1,6,256,256]{4,3,2,1,0:T(8,128)}, u32[]{:S(2)}) copy-start(s32[1,1,6,256,256]{4,3,2,1,0:T(8,128)} %param.11) | copy-start | bytes 4718596
  2.8 0.9 copy-start.2
  3.8 2.1 %copy-start.1 = (f32[2,256,256]{2,1,0:T(8,128)S(1)}, f32[2,256,256]{2,1,0:T(8,128)}, u32[]{:S(2)}) copy-start(f32[2,256,256]{2,1,0:T(8,128)} %field_ref.1) | copy-start | bytes 1572868
  5.8 18.1 %copy-start.3 = (f32[2,256,256]{2,1,0:T(8,128)S(1)}, f32[2,256,256]{2,1,0:T(8,128)}, u32[]{:S(2)}) copy-start(f32[2,256,256]{2,1,0:T(8,128)} %probe_ref.3) | copy-start | bytes 1572868
  5.9 18.1 %copy-start.4 = (bf16[2,4,256,256]{3,2,1,0:T(8,128)(2,1)S(1)}, bf16[2,4,256,256]{3,2,1,0:T(8,128)(2,1)}, u32[]{:S(2)}) copy-start(bf16[2,4,256,256]{3,2,1,0:T(8,128)(2,1)} %constant.4.clone.table_ref) | copy-start | bytes 3145732
